TPU v7x, 128 devices: a whole 4x4x4 slice. The times are simulated.
128 devices in a mesh: dp: 16 (over x_hi, z, core), blk: 8 (over y, x_lo).
Axes of the slice: x: 4 (x_hi: 2, x_lo: 2; x = x_hi * 2 + x_lo), y: 4, z: 4, core: 2. Of those that a mesh axis runs over, the one named last changes fastest.
Arguments:
- inputs: bfloat16 [512, 8192], P('blk', 'dp'), may hold values from -6 to 6
- upstream: bfloat16 [512, 8192], P('blk', 'dp'), may hold values from -1.5 to 1.5
- gate_weight: bfloat16 [8192, 14784], P('dp', 'blk'), may hold values from -0.0625 to 0.0625
- up_weight: bfloat16 [8192, 14784], P('dp', 'blk'), may hold values from -0.0625 to 0.0625
- down_weight: bfloat16 [14784, 8192], P('blk', 'dp'), may hold values from -0.046875 to 0.046875
Outputs:
- input_grad: bfloat16 [512, 8192], P('blk', 'dp')
- gate_grad: bfloat16 [8192, 14784], P('dp', 'blk')
- up_grad: bfloat16 [8192, 14784], P('dp', 'blk')
- down_grad: bfloat16 [14784, 8192], P('blk', 'dp')
All inputs are finite; a program needn't handle non-finite values.
Results may differ from a plain program's by a relative error of at most 0.005.
Values may be sent and summed in bfloat16 or wider, within the bound.
A program may use at most 128 MiB of HBM per device.

v0:
```python
import jax
import jax.numpy as jnp
from jax import lax
from jax.sharding import PartitionSpec as P


def contract_last(left, right):
    return lax.dot_general(
        left, right, (((1,), (1,)), ((), ())), preferred_element_type=jnp.float32
    )


def contract_first(left, right):
    return lax.dot_general(
        left, right, (((0,), (0,)), ((), ())), preferred_element_type=jnp.float32
    )


def elementwise(gate, up, back):
    sig = jax.nn.sigmoid(gate)
    hidden = (gate * sig * up).astype(jnp.bfloat16)
    up_delta = (back * gate * sig).astype(jnp.bfloat16)
    gate_delta = (back * up * sig * (1.0 + gate * (1.0 - sig))).astype(jnp.bfloat16)
    return (hidden, gate_delta, up_delta)


def local(inputs, upstream, gate_weight, up_weight, down_weight):
    both = lax.all_gather(jnp.concatenate([inputs, upstream], 1), "blk", axis=0, tiled=True)
    width = inputs.shape[1]
    rows_all, grads_all = (both[:, :width], both[:, width:])
    parts = [
        jnp.dot(rows_all, gate_weight, preferred_element_type=jnp.float32),
        jnp.dot(rows_all, up_weight, preferred_element_type=jnp.float32),
        contract_last(grads_all, down_weight),
    ]
    sums = [lax.psum_scatter(p, "dp", scatter_dimension=0, tiled=True) for p in parts]
    deltas = elementwise(*sums)
    hidden, gate_delta, up_delta = [lax.all_gather(d, "dp", axis=0, tiled=True) for d in deltas]
    partial_input = contract_last(gate_delta, gate_weight) + contract_last(up_delta, up_weight)
    parts = partial_input.reshape(8, -1, width)
    input_grad = jnp.sum(lax.all_to_all(parts, "blk", 0, 0, tiled=True), axis=0)
    down_grad = contract_first(hidden, grads_all).astype(jnp.bfloat16)
    gate_grad = contract_first(rows_all, gate_delta).astype(jnp.bfloat16)
    up_grad = contract_first(rows_all, up_delta).astype(jnp.bfloat16)
    return (input_grad.astype(jnp.bfloat16), gate_grad, up_grad, down_grad)


def solution(mesh):
    return jax.shard_map(
        local,
        mesh=mesh,
        in_specs=(P("blk", "dp"), P("blk", "dp"), P("dp", "blk"), P("dp", "blk"), P("blk", "dp")),
        out_specs=(P("blk", "dp"), P("dp", "blk"), P("dp", "blk"), P("blk", "dp")),
        check_vma=False,
    )
```

profile of v0, /device:TPU:1, one launch (start us, length us, event | category | flops | bytes accessed | tf_op | source)
XLA Modules:
  0.0 462.0 jit_solution(15373133980176718704)
XLA Ops:
  7.2 1.7 pad_maximum_fusion
  8.9 0.0 reduce-scatter.4.cloned.1.call-start
  9.0 39.6 %all-gather.5.cloned.1.call-done = bf16[512,1024]{1,0:T(8,128)(2,1)} async-done(((bf16[64,1024]{1,0:T(8,128)(2,1)}), bf16[512,1024]{1,0:T(8,128)(2,1)}) %all-gather.5.cloned.1.call-update) | async-done | bytes 1048592 | tf_op jit(solution)/shard_map/all_gather | solution.py:28
  48.6 4.8 %fusion.1 = f32[512,1848]{1,0:T(8,128)} fusion(bf16[1848,512]{1,0:T(8,128)(2,1)} %param.9, bf16[512,1024]{1,0:T(8,128)(2,1)} %all-gather.5.cloned.1.call-done), kind=kOutput, calls=%fused_computation.5 | convolution fusion | flops 968884224 | bytes 6201344 | tf_op jit(solution)/shard_map/dot_general | solution.py:8
  53.5 1.1 copy-done.1
  54.7 4.7 %fusion.7 = f32[512,1848]{1,0:T(8,128)} fusion(bf16[512,1848]{0,1:T(8,128)(2,1)} %param.8, bf16[512,1024]{1,0:T(8,128)(2,1)S(1)} %copy-done.1), kind=kOutput, calls=%fused_computation.11 | convolution fusion | flops 968884224 | bytes 6201344 | tf_op jit(solution)/shard_map/dot_general | solution.py:33
  59.4 3.3 fusion.5
  62.7 0.0 all-gather.7.cloned.1.call-start
  62.7 72.9 %reduce-scatter.4.cloned.1.call-done = f32[32,1848]{1,0:T(8,128)} async-done(((f32[512,1848]{1,0:T(8,128)}), f32[32,1848]{1,0:T(8,128)}) %reduce-scatter.4.cloned.1.call-update) | async-done | bytes 236560 | tf_op jit(solution)/shard_map/reduce_scatter | solution.py:36
  135.7 81.9 %reduce-scatter.6.cloned.1.call-done = f32[32,1848]{1,0:T(8,128)} async-done(((f32[512,1848]{1,0:T(8,128)}), f32[32,1848]{1,0:T(8,128)}) %reduce-scatter.6.cloned.1.call-update) | async-done | bytes 236560 | tf_op jit(solution)/shard_map/reduce_scatter | solution.py:36
  217.6 81.8 %reduce-scatter.8.cloned.1.call-done = f32[32,1848]{1,0:T(8,128)} async-done(((f32[512,1848]{1,0:T(8,128)}), f32[32,1848]{1,0:T(8,128)}) %reduce-scatter.8.cloned.1.call-update) | async-done | bytes 236560 | tf_op jit(solution)/shard_map/reduce_scatter | solution.py:36
  299.4 2.0 multiply_convert_fusion
  301.5 0.5 all-gather.9.cloned.1.call-update
  302.1 0.7 all-gather.11.cloned.1.call-update
  302.8 47.4 %all-gather.7.cloned.1.call-done = bf16[512,1848]{1,0:T(8,128)(2,1)} async-done(((bf16[32,1848]{1,0:T(8,128)(2,1)}), bf16[512,1848]{1,0:T(8,128)(2,1)}) %all-gather.7.cloned.1.call-update) | async-done | bytes 1892368 | tf_op jit(solution)/shard_map/all_gather | solution.py:38
  350.2 3.8 fusion.9
  354.0 45.2 %all-gather.9.cloned.1.call-done = bf16[512,1848]{1,0:T(8,128)(2,1)} async-done(((bf16[32,1848]{1,0:T(8,128)(2,1)}), bf16[512,1848]{1,0:T(8,128)(2,1)}) %all-gather.9.cloned.1.call-update) | async-done | bytes 1892368 | tf_op jit(solution)/shard_map/all_gather | solution.py:38
  399.2 4.6 convolution_add_fusion
  403.8 4.2 all-to-all-start
  408.0 4.2 convolution_convert_fusion.1
  412.2 2.4 convolution_convert_fusion.2
  414.6 34.6 %all-gather.11.cloned.1.call-done = bf16[512,1848]{1,0:T(8,128)(2,1)} async-done(((bf16[32,1848]{1,0:T(8,128)(2,1)}), bf16[512,1848]{1,0:T(8,128)(2,1)}) %all-gather.11.cloned.1.call-update) | async-done | bytes 1892368 | tf_op jit(solution)/shard_map/all_gather | solution.py:38
  449.2 4.0 convolution_convert_fusion
  453.2 1.9 reduce_sum.9
  (16 shorter events, 0.3 us)
Async XLA Ops:
  7.2 52.2 %copy-start = (bf16[512,1848]{0,1:T(8,128)(2,1)S(1)}, bf16[512,1848]{0,1:T(8,128)(2,1)}, u32[]{:S(2)}) copy-start(bf16[512,1848]{0,1:T(8,128)(2,1)} %param.7) | copy-start | bytes 5677060
  7.2 41.4 %all-gather.5.cloned.1.call-start = ((), (), s32[]{:S(2)}) async-start(), calls=%async_computation.4 | async-start | bytes 1179648 | tf_op jit(solution)/shard_map/all_gather | solution.py:28
  8.9 126.8 %reduce-scatter.4.cloned.1.call-start = ((), (), s32[]{:S(2)}) async-start(), calls=%async_computation.5 | async-start | bytes 4177920 | tf_op jit(solution)/shard_map/reduce_scatter | solution.py:36
  53.4 1.2 copy-start.1
  53.5 164.2 %reduce-scatter.6.cloned.1.call-start = ((), (), s32[]{:S(2)}) async-start(), calls=%async_computation.6 | async-start | bytes 4177920 | tf_op jit(solution)/shard_map/reduce_scatter | solution.py:36
  59.4 240.1 %reduce-scatter.8.cloned.1.call-start = ((), (), s32[]{:S(2)}) async-start(), calls=%async_computation.7 | async-start | bytes 4177920 | tf_op jit(solution)/shard_map/reduce_scatter | solution.py:36
  62.7 287.5 %all-gather.7.cloned.1.call-start = ((), (), s32[]{:S(2)}) async-start(), calls=%async_computation.8 | async-start | bytes 2088960 | tf_op jit(solution)/shard_map/all_gather | solution.py:38
  301.5 97.7 %all-gather.9.cloned.1.call-start = ((), (), s32[]{:S(2)}) async-start(), calls=%async_computation.9 | async-start | bytes 2088960 | tf_op jit(solution)/shard_map/all_gather | solution.py:38
  302.1 147.1 %all-gather.11.cloned.1.call-start = ((), (), s32[]{:S(2)}) async-start(), calls=%async_computation.10 | async-start | bytes 2088960 | tf_op jit(solution)/shard_map/all_gather | solution.py:38
  403.8 49.4 %all-to-all-start = ((f32[8,64,512]{2,1,0:T(8,128)}), f32[8,64,512]{2,1,0:T(8,128)}, u32[]{:S(2)}, u32[]{:S(2)}) async-start(f32[8,64,512]{2,1,0:T(8,128)} %bitcast.11), calls=%async_computation.3 | async-start | bytes 2097152 | tf_op jit(solution)/shard_map/all_to_all | solution.py:41
  408.0 4.2 copy-start.2
Sparse Core Ops, SparseCore 0:
  10.2 38.3 all-gather.4
  53.6 82.0 reduce-scatter.3
  139.8 77.7 reduce-scatter.5
  221.6 77.7 reduce-scatter.7
  302.3 47.8 all-gather.6
  353.1 46.0 all-gather.8
  401.7 47.4 all-gather.10
where the time goes:
time: 462 us
  waiting for transfers between devices  405 us (88%)
  matrix products  31.7 us (7%)
  between operations  14.2 us (3%)
  other arithmetic  5.63 us (1%)
    reduce_scatter x3, waiting for transfers between devices, local(): lax.psum_scatter(p, 'dp', scatter_dimension=0, tiled=True)  237 us
    all_gather x3, waiting for transfers between devices, local(): lax.all_gather(d, 'dp', axis=0, tiled=True)  127 us
    all_gather x1, waiting for transfers between devices, local(): lax.all_gather(jnp.concatenate([inputs, upstream], 1), 'blk', axis=0, til...  39.6 us
    dot_general x3, matrix products, contract_last(): lax.dot_general(left, right, (((1,), (1,)), ((), ())), preferred_element_...  13.2 us
    dot_general x3, matrix products, contract_first(): lax.dot_general(left, right, (((0,), (0,)), ((), ())), preferred_element_...  10.6 us
  transfers between devices with their start and end apart: 8, of which 7 were waited for; matrix products, arithmetic and copies ran while one was open for 6% of the time, Pallas kernels for 0%

commit v1 on v0

--- a/solution.py
+++ b/solution.py
@@ -2,6 +2,11 @@
 import jax.numpy as jnp
 from jax import lax
 from jax.sharding import PartitionSpec as P
+
+
+def exchange_gather(array, axis, d):
+    stack = jnp.stack([array] * lax.axis_size(axis))
+    return jnp.concatenate(lax.all_to_all(stack, axis, 0, 0), axis=d)
 
 
 def contract_last(left, right):
@@ -35,7 +40,7 @@
     ]
     sums = [lax.psum_scatter(p, "dp", scatter_dimension=0, tiled=True) for p in parts]
     deltas = elementwise(*sums)
-    hidden, gate_delta, up_delta = [lax.all_gather(d, "dp", axis=0, tiled=True) for d in deltas]
+    hidden, gate_delta, up_delta = [exchange_gather(d, "dp", 0) for d in deltas]
     partial_input = contract_last(gate_delta, gate_weight) + contract_last(up_delta, up_weight)
     parts = partial_input.reshape(8, -1, width)
     input_grad = jnp.sum(lax.all_to_all(parts, "blk", 0, 0, tiled=True), axis=0)

time: 462 us -> 429 us (0.929)
  waiting for transfers between devices: 405 us -> 302 us
  blocking collectives: 0 us -> 63.6 us
  starting transfers between devices: 4.53 us -> 10.7 us
    all_gather x3 -> x0, waiting for transfers between devices: 127 us -> none  [local(): lax.all_gather(d, 'dp', axis=0, tiled=True)]
    all_to_all x0 -> x2, blocking collectives: none -> 63.6 us  [exchange_gather(): return jnp.concatenate(lax.all_to_all(stack, axis, 0, 0), axis=d)]
    all_to_all x0 -> x1, waiting for transfers between devices: none -> 21.8 us  [exchange_gather(): return jnp.concatenate(lax.all_to_all(stack, axis, 0, 0), axis=d)]
    all_to_all x0 -> x1, starting transfers between devices: none -> 5.42 us  [exchange_gather(): return jnp.concatenate(lax.all_to_all(stack, axis, 0, 0), axis=d)]
  transfers between devices with their start and end apart: 8 -> 6, of which waited for: 7 -> 6; matrix products, arithmetic and copies ran while one was open for 6% -> 6% of each run, Pallas kernels for 0% -> 0%
where the time goes in v1:
time: 429 us; the launch traced here: 427 us
  waiting for transfers between devices  302 us (70%)
  blocking collectives  63.6 us (15%)
  matrix products  28.6 us (7%)
  between operations  13.8 us (3%)
  starting transfers between devices  10.7 us (2%)
  other arithmetic  4.93 us (1%)
    reduce_scatter x3, waiting for transfers between devices, local(): lax.psum_scatter(p, 'dp', scatter_dimension=0, tiled=True)  237 us
    all_to_all x2, blocking collectives, exchange_gather(): return jnp.concatenate(lax.all_to_all(stack, axis, 0, 0), axis=d)  63.6 us
    all_gather x1, waiting for transfers between devices, local(): lax.all_gather(jnp.concatenate([inputs, upstream], 1), 'blk', axis=0, til...  39.6 us
    all_to_all x1, waiting for transfers between devices, exchange_gather(): return jnp.concatenate(lax.all_to_all(stack, axis, 0, 0), axis=d)  21.8 us
    dot_general x3, matrix products, contract_first(): lax.dot_general(left, right, (((0,), (0,)), ((), ())), preferred_element_...  10.6 us
    dot_general x3, matrix products, contract_last(): lax.dot_general(left, right, (((1,), (1,)), ((), ())), preferred_element_...  10.1 us
  transfers between devices with their start and end apart: 6, of which 6 were waited for; matrix products, arithmetic and copies ran while one was open for 6% of the time, Pallas kernels for 0%

profile of v1, /device:TPU:1, one launch (start us, length us, event | category | flops | bytes accessed | tf_op | source)
XLA Modules:
  0.0 426.5 jit_solution(295176259943262406)
XLA Ops:
  7.2 1.7 pad_maximum_fusion
  9.0 39.6 %all-gather.2.cloned.1.call-done = bf16[512,1024]{1,0:T(8,128)(2,1)} async-done(((bf16[64,1024]{1,0:T(8,128)(2,1)}), bf16[512,1024]{1,0:T(8,128)(2,1)}) %all-gather.2.cloned.1.call-update) | async-done | bytes 1048592 | tf_op jit(solution)/shard_map/all_gather | solution.py:33
  48.6 4.8 %fusion.1 = f32[512,1848]{1,0:T(8,128)} fusion(bf16[1848,512]{1,0:T(8,128)(2,1)} %param.9, bf16[512,1024]{1,0:T(8,128)(2,1)} %all-gather.2.cloned.1.call-done), kind=kOutput, calls=%fused_computation.5 | convolution fusion | flops 968884224 | bytes 6201344 | tf_op jit(solution)/shard_map/dot_general | solution.py:13
  53.5 1.1 copy-done.1
  54.7 4.7 %fusion.7 = f32[512,1848]{1,0:T(8,128)} fusion(bf16[512,1848]{0,1:T(8,128)(2,1)} %param.8, bf16[512,1024]{1,0:T(8,128)(2,1)S(1)} %copy-done.1), kind=kOutput, calls=%fused_computation.11 | convolution fusion | flops 968884224 | bytes 6201344 | tf_op jit(solution)/shard_map/dot_general | solution.py:38
  59.5 3.3 fusion.5
  62.8 73.0 %reduce-scatter.4.cloned.1.call-done = f32[32,1848]{1,0:T(8,128)} async-done(((f32[512,1848]{1,0:T(8,128)}), f32[32,1848]{1,0:T(8,128)}) %reduce-scatter.4.cloned.1.call-update) | async-done | bytes 236560 | tf_op jit(solution)/shard_map/reduce_scatter | solution.py:41
  135.7 81.9 %reduce-scatter.6.cloned.1.call-done = f32[32,1848]{1,0:T(8,128)} async-done(((f32[512,1848]{1,0:T(8,128)}), f32[32,1848]{1,0:T(8,128)}) %reduce-scatter.6.cloned.1.call-update) | async-done | bytes 236560 | tf_op jit(solution)/shard_map/reduce_scatter | solution.py:41
  217.6 81.8 %reduce-scatter.8.cloned.1.call-done = f32[32,1848]{1,0:T(8,128)} async-done(((f32[512,1848]{1,0:T(8,128)}), f32[32,1848]{1,0:T(8,128)}) %reduce-scatter.8.cloned.1.call-update) | async-done | bytes 236560 | tf_op jit(solution)/shard_map/reduce_scatter | solution.py:41
  299.5 1.3 multiply_convert_fusion
  300.8 0.1 stack.6
  300.9 32.5 %all_to_all.20 = bf16[16,32,1848]{2,1,0:T(8,128)(2,1)} all-to-all(bf16[16,32,1848]{2,1,0:T(8,128)(2,1)S(1)} %stack.6), channel_id=1, replica_groups=mesh['dp'=16,'blk'=8] {'dp'}, dimensions={0} | all-to-all | bytes 3784704 | tf_op jit(solution)/shard_map/all_to_all | solution.py:9
  333.5 31.1 %all_to_all.21 = bf16[16,32,1848]{2,1,0:T(8,128)(2,1)} all-to-all(bf16[16,32,1848]{2,1,0:T(8,128)(2,1)S(1)} %stack.7), channel_id=1, replica_groups=mesh['dp'=16,'blk'=8] {'dp'}, dimensions={0} | all-to-all | bytes 3784704 | tf_op jit(solution)/shard_map/all_to_all | solution.py:9
  364.6 1.4 stack.8
  366.1 5.4 %all-to-all-start.3 = ((bf16[16,32,1848]{2,1,0:T(8,128)(2,1)}), bf16[16,32,1848]{2,1,0:T(8,128)(2,1)}, u32[]{:S(2)}, u32[]{:S(2)}) async-start(bf16[16,32,1848]{2,1,0:T(8,128)(2,1)} %stack.8), calls=%async_computation.6 | async-start | bytes 3932160 | tf_op jit(solution)/shard_map/all_to_all | solution.py:9
  371.5 2.9 fusion.9
  374.5 2.3 convolution_add_fusion
  376.8 21.8 %all-to-all-done.3 = bf16[16,32,1848]{2,1,0:T(8,128)(2,1)} async-done(((bf16[16,32,1848]{2,1,0:T(8,128)(2,1)}), bf16[16,32,1848]{2,1,0:T(8,128)(2,1)}, u32[]{:S(2)}, u32[]{:S(2)}) %all-to-all-start.3) | async-done | bytes 1892384 | tf_op jit(solution)/shard_map/all_to_all | solution.py:9
  398.6 5.1 %all-to-all-start.2 = ((f32[8,64,512]{2,1,0:T(8,128)}), f32[8,64,512]{2,1,0:T(8,128)}, u32[]{:S(2)}, u32[]{:S(2)}) async-start(f32[8,64,512]{2,1,0:T(8,128)} %bitcast.18), calls=%async_computation.5 | async-start | bytes 2097152 | tf_op jit(solution)/shard_map/all_to_all | solution.py:46
  403.8 4.1 convolution_convert_fusion.1
  407.9 2.5 convolution_convert_fusion.2
  410.4 4.0 convolution_convert_fusion
  414.3 3.7 all-to-all-done.2
  418.1 1.9 reduce_sum.9
  (18 shorter events, 0.4 us)
Async XLA Ops:
  7.2 52.3 %copy-start = (bf16[512,1848]{0,1:T(8,128)(2,1)S(1)}, bf16[512,1848]{0,1:T(8,128)(2,1)}, u32[]{:S(2)}) copy-start(bf16[512,1848]{0,1:T(8,128)(2,1)} %param.7) | copy-start | bytes 5677060
  7.2 41.4 %all-gather.2.cloned.1.call-start = ((), (), s32[]{:S(2)}) async-start(), calls=%async_computation.7 | async-start | bytes 1179648 | tf_op jit(solution)/shard_map/all_gather | solution.py:33
  8.9 126.8 %reduce-scatter.4.cloned.1.call-start = ((), (), s32[]{:S(2)}) async-start(), calls=%async_computation.8 | async-start | bytes 4177920 | tf_op jit(solution)/shard_map/reduce_scatter | solution.py:41
  53.5 1.2 copy-start.1
  53.5 164.2 %reduce-scatter.6.cloned.1.call-start = ((), (), s32[]{:S(2)}) async-start(), calls=%async_computation.9 | async-start | bytes 4177920 | tf_op jit(solution)/shard_map/reduce_scatter | solution.py:41
  59.4 240.1 %reduce-scatter.8.cloned.1.call-start = ((), (), s32[]{:S(2)}) async-start(), calls=%async_computation.10 | async-start | bytes 4177920 | tf_op jit(solution)/shard_map/reduce_scatter | solution.py:41
  366.1 32.6 %all-to-all-start.3 = ((bf16[16,32,1848]{2,1,0:T(8,128)(2,1)}), bf16[16,32,1848]{2,1,0:T(8,128)(2,1)}, u32[]{:S(2)}, u32[]{:S(2)}) async-start(bf16[16,32,1848]{2,1,0:T(8,128)(2,1)} %stack.8), calls=%async_computation.6 | async-start | bytes 3932160 | tf_op jit(solution)/shard_map/all_to_all | solution.py:9
  371.5 3.0 copy-start.3
  371.5 3.0 copy-start.4
  398.6 19.4 %all-to-all-start.2 = ((f32[8,64,512]{2,1,0:T(8,128)}), f32[8,64,512]{2,1,0:T(8,128)}, u32[]{:S(2)}, u32[]{:S(2)}) async-start(f32[8,64,512]{2,1,0:T(8,128)} %bitcast.18), calls=%async_computation.5 | async-start | bytes 2097152 | tf_op jit(solution)/shard_map/all_to_all | solution.py:46
  403.8 4.1 copy-start.2
Sparse Core Ops, SparseCore 0:
  10.2 38.3 all-gather.1
  53.6 82.0 reduce-scatter.3
  139.9 77.7 reduce-scatter.5
  221.6 77.7 reduce-scatter.7
